TPU v7x, 256 devices: a whole 4x4x8 slice. The times are simulated.
256 devices in a mesh: atom: 32 (over x_lo, z, core), freq: 8 (over x_hi, y).
Axes of the slice: x: 4 (x_hi: 2, x_lo: 2; x = x_hi * 2 + x_lo), y: 4, z: 8, core: 2. Of those that a mesh axis runs over, the one named last changes fastest.
Arguments:
- feats: bfloat16 [65536, 256], P('atom'), may hold values from -6 to 6
- positions: float32 [3, 65536], P(None, 'atom'), may hold values from 0 to 2
- phases: bfloat16 [2, 65536, 1024], P(None, 'atom', 'freq')
- filt: float32 [1024, 256], P('freq'), may hold values from 0.3 to 3
- w_value: bfloat16 [256, 256], replicated, may hold values from -0.375 to 0.375
- neighbour_tiles: int32 [512, 8], P(('atom', 'freq')), may hold values from 0 to 511, as said below
- neighbour_count: int32 [512], P(('atom', 'freq')), may hold values from 1 to 8, as said below
Outputs:
- updated: bfloat16 [65536, 256], P(('atom', 'freq'))
Inputs may be any that keep to these rules, and one draw needn't show every extreme that they name: `neighbour_tiles`: a tile's entries are distinct tiles of its own block of 16 tiles (tiles b * 16 to (b + 1) * 16 - 1) or of the block just before or after it, counted around the ends. `neighbour_count`: some tile has 8.
All inputs are finite; a program needn't handle non-finite values.
Results may differ from a plain program's by a relative error of at most 0.0095.
Values may be sent and summed in bfloat16 or wider, within the bound.
A program may use at most 64 MiB of HBM per device.

v0:
```python
import math

import jax
import jax.numpy as jnp
from jax import lax
from jax.sharding import PartitionSpec as P

TILE = 128


def in_blocks(value, dim, size):
    shape = value.shape
    blocks = value.reshape(*shape[:dim], size, shape[dim] // size, *shape[dim + 1 :])
    return jnp.moveaxis(blocks, dim, 0)


def sum_at_owner(value, axis, dim):
    blocks = in_blocks(value, dim, lax.axis_size(axis))
    arrived = lax.all_to_all(blocks, axis, split_axis=0, concat_axis=0, tiled=True)
    return arrived.sum(axis=0)


def from_everyone(value, axis):
    size = lax.axis_size(axis)
    return lax.all_to_all(
        jnp.broadcast_to(value[None], (size, *value.shape)), axis, 0, 0, tiled=True
    )


def in_order(blocks, dim):
    blocks = jnp.moveaxis(blocks, 0, dim)
    shape = blocks.shape
    return blocks.reshape(*shape[:dim], shape[dim] * shape[dim + 1], *shape[dim + 2 :])


def collect(value, axis, dim):
    blocks = from_everyone(value, axis)
    return in_order(blocks, dim)


def sum_at_owner_2(value, axis, dim):
    size = lax.axis_size(axis)
    blocks = lax.all_to_all(in_blocks(value, dim, size), axis, 0, 0, tiled=True)
    return jnp.sum(blocks.astype(jnp.float32), axis=0)


def with_halo(cells, sides, width):
    for axis, dim in sides:
        count = lax.axis_size(axis)
        head = lax.slice_in_dim(cells, 0, width, axis=dim)
        tail = lax.slice_in_dim(cells, cells.shape[dim] - width, cells.shape[dim], axis=dim)
        cells = jnp.concatenate(
            [
                lax.ppermute(tail, axis, [(i, (i + 1) % count) for i in range(count)]),
                cells,
                lax.ppermute(head, axis, [((i + 1) % count, i) for i in range(count)]),
            ],
            axis=dim,
        )
    return cells


def shards(feats, positions, phases, filt, w_value, neighbour_tiles, neighbour_count):
    n_atom = lax.axis_size("atom")
    n_freq = lax.axis_size("freq")
    me_atom = lax.axis_index("atom")
    me_freq = lax.axis_index("freq")
    block_rows, width = feats.shape
    rows = block_rows // n_freq
    tiles_dev = block_rows // TILE
    tiles_here = rows // TILE
    freq_local = phases.shape[2]
    scale = 1.0 / math.sqrt(block_rows * n_atom * freq_local * n_freq)
    partial_sf = lax.dot_general(
        phases, feats, (((1,), (0,)), ((), ())), preferred_element_type=jnp.float32
    )
    share = sum_at_owner(partial_sf, "atom", 1)
    span = share.shape[1]
    filt_share = lax.dynamic_slice_in_dim(filt, me_atom * span, span, 0)
    filtered = collect((filt_share[None] * share * scale).astype(jnp.bfloat16), "atom", 1)
    row_start = me_freq * rows
    long_msg = sum_at_owner_2(
        (
            jnp.dot(phases[0], filtered[0], preferred_element_type=jnp.float32)
            + jnp.dot(phases[1], filtered[1], preferred_element_type=jnp.float32)
        ).astype(jnp.bfloat16),
        "freq",
        0,
    )
    own_feats = lax.dynamic_slice_in_dim(feats, row_start, rows, 0)
    own_positions = lax.dynamic_slice_in_dim(positions, row_start, rows, 1)
    values = jnp.dot(feats, w_value, preferred_element_type=jnp.float32).astype(jnp.bfloat16)
    near_values = with_halo(values, (("atom", 0),), block_rows)
    near_centres = with_halo(positions, (("atom", 1),), block_rows)
    v_tiles = near_values.reshape(3 * tiles_dev, TILE, width)
    p_tiles = near_centres.reshape(3, 3 * tiles_dev, TILE)
    home_block = neighbour_tiles // tiles_dev
    relative = (home_block - me_atom + 1 + n_atom) % n_atom
    local_ids = relative * tiles_dev + neighbour_tiles % tiles_dev
    near_v = v_tiles[local_ids]
    near_p = p_tiles[:, local_ids]
    own_pos = own_positions.reshape(3, tiles_here, TILE)
    dist = jnp.zeros((tiles_here, TILE, neighbour_tiles.shape[1], TILE), jnp.float32)
    for axis_c in range(3):
        diff = own_pos[axis_c][:, :, None, None] - near_p[axis_c][:, None, :, :]
        dist = dist + diff * diff
    live = (
        jnp.arange(neighbour_tiles.shape[1], dtype=jnp.int32)[None, :] < neighbour_count[:, None]
    ).astype(jnp.float32)
    weight = (jnp.exp(-dist) * live[:, None, :, None]).astype(jnp.bfloat16)
    short = jnp.einsum("tinj,tnjc->tic", weight, near_v, preferred_element_type=jnp.float32)
    short_msg = short.reshape(rows, width) / math.sqrt(TILE)
    return (own_feats.astype(jnp.float32) + long_msg + short_msg).astype(jnp.bfloat16)


def solution(mesh):
    in_specs = (
        P("atom", None),
        P(None, "atom"),
        P(None, "atom", "freq"),
        P("freq", None),
        P(),
        P(("atom", "freq"), None),
        P(("atom", "freq")),
    )
    out_specs = P(("atom", "freq"), None)
    return jax.shard_map(shards, mesh=mesh, in_specs=in_specs, out_specs=out_specs, check_vma=False)
```

profile of v0, /device:TPU:8, one launch (start us, length us, event | category | flops | bytes accessed | tf_op | source)
XLA Modules:
  0.0 74.3 jit_solution(2085783994432085018)
XLA Ops:
  0.0 1.2 %copy-done = bf16[2048,256]{1,0:T(8,128)(2,1)S(1)} copy-done((bf16[2048,256]{1,0:T(8,128)(2,1)S(1)}, bf16[2048,256]{1,0:T(8,128)(2,1)}, u32[]{:S(2)}) %copy-start) | copy-done | bytes 1048600
  1.2 1.4 %convolution_convert_fusion = bf16[2048,256]{1,0:T(8,128)(2,1)S(1)} fusion(bf16[2048,256]{1,0:T(8,128)(2,1)S(1)} %copy-done, bf16[256,256]{1,0:T(8,128)(2,1)} %param.11), kind=kOutput, calls=%fused_computation.5 | convolution fusion | flops 268959744 | bytes 2228224 | tf_op jit(solution)/shard_map/dot_general | solution.py:92
  2.6 6.3 %collective-permute-start.3 = (bf16[2048,256]{1,0:T(8,128)(2,1)S(1)}, bf16[2048,256]{1,0:T(8,128)(2,1)}, u32[]{:S(2)}, u32[]{:S(2)}) collective-permute-start(bf16[2048,256]{1,0:T(8,128)(2,1)S(1)} %convolution_convert_fusion), channel_id=1, source_target_pairs={{8,0},{16,8},{24,16},{32,24},{40,32},{48,40},{56,48},{64,56},{72,6... | collective-permute-start | bytes 3145736 | tf_op jit(solution)/shard_map/ppermute | solution.py:56
  8.9 3.9 %collective-permute-start.1 = (f32[3,2048]{1,0:T(4,128)}, f32[3,2048]{1,0:T(4,128)}, u32[]{:S(2)}, u32[]{:S(2)}) collective-permute-start(f32[3,2048]{1,0:T(4,128)} %param.8), channel_id=1, source_target_pairs={{8,0},{16,8},{24,16},{32,24},{40,32},{48,40},{56,48},{64,56},{72,6... | collective-permute-start | bytes 73736 | tf_op jit(solution)/shard_map/ppermute | solution.py:56
  12.8 1.7 %fusion.2 = f32[2,128,256]{2,1,0:T(8,128)S(1)} fusion(bf16[2,2048,128]{2,1,0:T(8,128)(2,1)} %param.9, bf16[2048,256]{1,0:T(8,128)(2,1)S(1)} %copy-done), kind=kOutput, calls=%fused_computation.10 | convolution fusion | flops 268435456 | bytes 2359296 | tf_op jit(solution)/shard_map/dot_general | solution.py:74
  14.4 0.8 %reshape.60 = f32[2,32,4,256]{3,2,1,0:T(4,128)} reshape(f32[2,128,256]{2,1,0:T(8,128)S(1)} %fusion.2) | data formatting | bytes 524288 | tf_op jit(solution)/shard_map/reshape | solution.py:13
  15.2 1.7 %copy.25 = f32[2,32,4,256]{3,2,0,1:T(4,128)} copy(f32[2,32,4,256]{3,2,1,0:T(4,128)} %reshape.60) | data formatting | bytes 524288 | tf_op jit(solution)/shard_map/reshape | solution.py:13
  16.9 5.5 %all-to-all-start = ((f32[32,2,4,256]{3,2,1,0:T(4,128)}), f32[32,2,4,256]{3,2,1,0:T(4,128)S(1)}, u32[]{:S(2)}, u32[]{:S(2)}) async-start(f32[32,2,4,256]{3,2,1,0:T(4,128)} %bitcast.49), calls=%async_computation | async-start | bytes 524288 | tf_op jit(solution)/shard_map/all_to_all | solution.py:19
  22.6 0.8 %copy.20 = bf16[256,256]{0,1:T(8,128)(2,1)} copy(bf16[256,256]{1,0:T(8,128)(2,1)S(1)} %constant_dynamic-slice_fusion.2) | data formatting | bytes 262144
  23.3 1.5 %constant_dynamic-slice_fusion = (f32[1,256]{1,0:T(1,128)}, f32[1,256]{1,0:T(1,128)}, f32[1,256]{1,0:T(1,128)}) fusion(f32[3,2048]{1,0:T(4,128)} %param.8, s32[]{:T(128)S(6)} %select_n.27, s32[]{:T(128)S(6)} %add.62, s32[]{:T(128)S(6)} %add.63), kind=kLoop, calls=%fused_computation.43 | loop fusion | bytes 6156 | tf_op jit(solution)/shard_map/slice | solution.py:105
  24.8 0.7 constant_dynamic-slice_fusion.1
  25.5 0.7 compare_convert_fusion
  26.2 9.4 %all-to-all-done = f32[32,2,4,256]{3,2,1,0:T(4,128)S(1)} async-done(((f32[32,2,4,256]{3,2,1,0:T(4,128)}), f32[32,2,4,256]{3,2,1,0:T(4,128)S(1)}, u32[]{:S(2)}, u32[]{:S(2)}) %all-to-all-start) | async-done | bytes 262176 | tf_op jit(solution)/shard_map/all_to_all | solution.py:19
  35.7 0.7 broadcast_in_dim.4
  36.4 3.9 %all-to-all-start.1 = ((bf16[32,2,4,256]{3,2,1,0:T(4,128)(2,1)}), bf16[32,2,4,256]{3,2,1,0:T(4,128)(2,1)S(1)}, u32[]{:S(2)}, u32[]{:S(2)}) async-start(bf16[32,2,4,256]{3,2,1,0:T(4,128)(2,1)} %broadcast_in_dim.4), calls=%async_computation.1 | async-start | bytes 262144 | tf_op jit(solution)/shard_map/all_to_all | solution.py:25
  40.2 0.8 %maximum_bitcast_fusion = f32[3,48,128]{2,0,1:T(4,128)S(1)} fusion(f32[3,2048]{1,0:T(4,128)} %collective-permute-done.1, f32[3,2048]{1,0:T(4,128)} %param.8, f32[3,2048]{1,0:T(4,128)} %collective-permute-done), kind=kLoop, calls=%fused_computation.27 | loop fusion | flops 36864 | bytes 147456 | tf_op jit(solution)/shard_map/reshape | solution.py:96
  42.3 8.4 %all-to-all-done.1 = bf16[32,2,4,256]{3,2,1,0:T(4,128)(2,1)S(1)} async-done(((bf16[32,2,4,256]{3,2,1,0:T(4,128)(2,1)}), bf16[32,2,4,256]{3,2,1,0:T(4,128)(2,1)S(1)}, u32[]{:S(2)}, u32[]{:S(2)}) %all-to-all-start.1) | async-done | bytes 131104 | tf_op jit(solution)/shard_map/all_to_all | solution.py:25
  51.7 1.1 %copy.24 = bf16[32,8,8,256]{3,2,0,1:T(8,128)(2,1)} copy(bf16[32,8,8,256]{3,2,1,0:T(8,128)(2,1)S(1)} %bitcast.48) | data formatting | bytes 2097152 | tf_op jit(solution)/shard_map/reshape | solution.py:13
  52.7 7.1 %all-to-all-start.2 = ((bf16[8,256,256]{1,2,0:T(8,128)(2,1)}), bf16[8,256,256]{1,2,0:T(8,128)(2,1)S(1)}, u32[]{:S(2)}, u32[]{:S(2)}) async-start(bf16[8,256,256]{1,2,0:T(8,128)(2,1)} %bitcast.45), calls=%async_computation.2 | async-start | bytes 2097152 | tf_op jit(solution)/shard_map/all_to_all | solution.py:43
  59.8 3.0 %pad_maximum_fusion = bf16[6144,256]{1,0:T(8,128)(2,1)} fusion(bf16[2048,256]{1,0:T(8,128)(2,1)} %collective-permute-done.3, bf16[2048,256]{1,0:T(8,128)(2,1)S(1)} %convolution_convert_fusion, bf16[2048,256]{1,0:T(8,128)(2,1)} %collective-permute-done.2), kind=kLoop, calls=%fused_computation.2 | loop fusion | flops 9437184 | bytes 6291456 | tf_op jit(solution)/shard_map/concatenate | solution.py:52
  62.8 2.5 %gather_fusion.1 = bf16[16,128,256]{2,1,0:T(8,128)(2,1)S(1)} fusion(bf16[48,128,256]{2,1,0:T(8,128)(2,1)} %bitcast.47, s32[1024]{0:T(1024)S(1)} %pad_clamp_fusion), kind=kCustom, calls=%fused_computation.1 | custom fusion | bytes 2097216 | tf_op jit(solution)/shard_map/gather | solution.py:100
  65.4 1.4 %fusion.1 = f32[2,128,256]{2,1,0:T(8,128)S(1)} fusion(bf16[2,8,128,256]{3,2,1,0:T(8,128)(2,1)S(1)} %bitcast.50, f32[2,8]{1,0:T(2,128)} %compare_convert_fusion, f32[2,8,128]{2,1,0:T(8,128)} %bitcast.56, f32[2,128]{1,0:T(2,128)} %bitcast.59, f32[2,8,128]{2,1,0:T(8,128)S(1)} %bitcast.55, f32[2,128]{1,0:T(2,128)} %bitcast.58, f32[2,8,128]{2,1,0:T(8,128)S(1)} %bitcast.54, ...), kind=kOutput, calls=%fused_computation.8 | convolution fusion | flops 137166848 | bytes 1338432 | tf_op jit(solution)/shard_map/tinj,tnjc->tic/dot_general | solution.py:111
  66.9 6.5 %all-to-all-done.2 = bf16[8,256,256]{1,2,0:T(8,128)(2,1)S(1)} async-done(((bf16[8,256,256]{1,2,0:T(8,128)(2,1)}), bf16[8,256,256]{1,2,0:T(8,128)(2,1)S(1)}, u32[]{:S(2)}, u32[]{:S(2)}) %all-to-all-start.2) | async-done | bytes 1048608 | tf_op jit(solution)/shard_map/all_to_all | solution.py:43
  73.6 0.8 %copy.16 = bf16[256,256]{1,0:T(8,128)(2,1)} copy(bf16[256,256]{0,1:T(8,128)(2,1)S(1)} %add_convert_fusion) | data formatting | bytes 262144 | tf_op jit(solution)/shard_map/convert_element_type | solution.py:113
  (31 shorter events, 2.8 us)
Async XLA Ops:
  0.0 1.2 %copy-start = (bf16[2048,256]{1,0:T(8,128)(2,1)S(1)}, bf16[2048,256]{1,0:T(8,128)(2,1)}, u32[]{:S(2)}) copy-start(bf16[2048,256]{1,0:T(8,128)(2,1)} %param.7) | copy-start | bytes 3145732
  0.0 22.4 %copy-start.3 = (s32[2,8]{1,0:T(2,128)S(1)}, s32[2,8]{1,0:T(2,128)}, u32[]{:S(2)}) copy-start(s32[2,8]{1,0:T(2,128)} %param.12) | copy-start | bytes 196
  1.2 24.3 %copy-start.4 = (s32[2]{0:T(128)S(1)}, s32[2]{0:T(128)}, u32[]{:S(2)}) copy-start(s32[2]{0:T(128)} %param.13) | copy-start | bytes 28
  2.6 48.2 %copy-start.1 = (bf16[2,2048,128]{2,1,0:T(8,128)(2,1)S(1)}, bf16[2,2048,128]{2,1,0:T(8,128)(2,1)}, u32[]{:S(2)}) copy-start(bf16[2,2048,128]{2,1,0:T(8,128)(2,1)} %param.9) | copy-start | bytes 3145732
  2.6 57.2 %collective-permute-start.3 = (bf16[2048,256]{1,0:T(8,128)(2,1)S(1)}, bf16[2048,256]{1,0:T(8,128)(2,1)}, u32[]{:S(2)}, u32[]{:S(2)}) collective-permute-start(bf16[2048,256]{1,0:T(8,128)(2,1)S(1)} %convolution_convert_fusion), channel_id=1, source_target_pairs={{8,0},{16,8},{24,16},{32,24},{40,32},{48,40},{56,48},{64,56},{72,6... | collective-permute-start | bytes 3145736 | tf_op jit(solution)/shard_map/ppermute | solution.py:56
  8.9 50.9 %collective-permute-start.2 = (bf16[2048,256]{1,0:T(8,128)(2,1)S(1)}, bf16[2048,256]{1,0:T(8,128)(2,1)}, u32[]{:S(2)}, u32[]{:S(2)}) collective-permute-start(bf16[2048,256]{1,0:T(8,128)(2,1)S(1)} %convolution_convert_fusion), channel_id=1, source_target_pairs={{0,8},{8,16},{16,24},{24,32},{32,40},{40,48},{48,56},{56,64},{64,7... | collective-permute-start | bytes 3145736 | tf_op jit(solution)/shard_map/ppermute | solution.py:54
  8.9 31.3 %collective-permute-start.1 = (f32[3,2048]{1,0:T(4,128)}, f32[3,2048]{1,0:T(4,128)}, u32[]{:S(2)}, u32[]{:S(2)}) collective-permute-start(f32[3,2048]{1,0:T(4,128)} %param.8), channel_id=1, source_target_pairs={{8,0},{16,8},{24,16},{32,24},{40,32},{48,40},{56,48},{64,56},{72,6... | collective-permute-start | bytes 73736 | tf_op jit(solution)/shard_map/ppermute | solution.py:56
  12.7 27.5 %collective-permute-start = (f32[3,2048]{1,0:T(4,128)}, f32[3,2048]{1,0:T(4,128)}, u32[]{:S(2)}, u32[]{:S(2)}) collective-permute-start(f32[3,2048]{1,0:T(4,128)} %param.8), channel_id=1, source_target_pairs={{0,8},{8,16},{16,24},{24,32},{32,40},{40,48},{48,56},{56,64},{64,7... | collective-permute-start | bytes 73736 | tf_op jit(solution)/shard_map/ppermute | solution.py:54
  16.9 18.7 %all-to-all-start = ((f32[32,2,4,256]{3,2,1,0:T(4,128)}), f32[32,2,4,256]{3,2,1,0:T(4,128)S(1)}, u32[]{:S(2)}, u32[]{:S(2)}) async-start(f32[32,2,4,256]{3,2,1,0:T(4,128)} %bitcast.49), calls=%async_computation | async-start | bytes 524288 | tf_op jit(solution)/shard_map/all_to_all | solution.py:19
  36.4 14.3 %all-to-all-start.1 = ((bf16[32,2,4,256]{3,2,1,0:T(4,128)(2,1)}), bf16[32,2,4,256]{3,2,1,0:T(4,128)(2,1)S(1)}, u32[]{:S(2)}, u32[]{:S(2)}) async-start(bf16[32,2,4,256]{3,2,1,0:T(4,128)(2,1)} %broadcast_in_dim.4), calls=%async_computation.1 | async-start | bytes 262144 | tf_op jit(solution)/shard_map/all_to_all | solution.py:25
  52.7 20.6 %all-to-all-start.2 = ((bf16[8,256,256]{1,2,0:T(8,128)(2,1)}), bf16[8,256,256]{1,2,0:T(8,128)(2,1)S(1)}, u32[]{:S(2)}, u32[]{:S(2)}) async-start(bf16[8,256,256]{1,2,0:T(8,128)(2,1)} %bitcast.45), calls=%async_computation.2 | async-start | bytes 2097152 | tf_op jit(solution)/shard_map/all_to_all | solution.py:43
  65.4 8.2 %copy-start.2 = (bf16[256,256]{0,1:T(8,128)(2,1)S(1)}, bf16[256,256]{0,1:T(8,128)(2,1)}, u32[]{:S(2)}) copy-start(bf16[256,256]{0,1:T(8,128)(2,1)} %copy.20) | copy-start | bytes 393220
where the time goes:
time: 75 us; the launch traced here: 74.3 us
  starting transfers between devices  26.6 us (35%)
  waiting for transfers between devices  24.3 us (32%)
  local copies, waits for them, and re-layouts  13.1 us (17%)
  matrix products  5.32 us (7%)
  other arithmetic  4.76 us (6%)
    ppermute x2, starting transfers between devices, with_halo(): lax.ppermute(head, axis, [((i + 1) % count, i) for i in range(count)])  10.1 us
    all_to_all x1, waiting for transfers between devices, sum_at_owner(): lax.all_to_all(blocks, axis, split_axis=0, concat_axis=0, tiled=True)  9.43 us
    all_to_all x1, waiting for transfers between devices, from_everyone(): lax.all_to_all(jnp.broadcast_to(value[None], (size, *value.shape)), axis,...  8.38 us
    all_to_all x1, starting transfers between devices, sum_at_owner_2(): blocks = lax.all_to_all(in_blocks(value, dim, size), axis, 0, 0, tiled=True)  7.1 us
    all_to_all x1, waiting for transfers between devices, sum_at_owner_2(): blocks = lax.all_to_all(in_blocks(value, dim, size), axis, 0, 0, tiled=True)  6.51 us
    all_to_all x1, starting transfers between devices, sum_at_owner(): lax.all_to_all(blocks, axis, split_axis=0, concat_axis=0, tiled=True)  5.52 us
    all_to_all x1, starting transfers between devices, from_everyone(): lax.all_to_all(jnp.broadcast_to(value[None], (size, *value.shape)), axis,...  3.86 us
    reshape x3, local copies, waits for them, and re-layouts, in_blocks(): value.reshape(*shape[:dim], size, shape[dim] // size, *shape[dim + 1:])  3.52 us
  transfers between devices with their start and end apart: 7, of which 3 were waited for; matrix products, arithmetic and copies ran while one was open for 27% of the time, Pallas kernels for 0%

commit v1 on v0

v1 whole, which is shorter than its diff:
```python
import functools
import math

import jax
import jax.numpy as jnp
from jax import lax
from jax.experimental import pallas as pl
from jax.experimental.pallas import tpu as pltpu
from jax.sharding import PartitionSpec as P

MESH = pl.DeviceIdType.MESH
TILE = 128
CHUNKS = 4
FIRST = 448
FAR = 1e30

F32 = jnp.float32
BF16 = jnp.bfloat16


def dot(a, b):
    return jnp.dot(a, b, preferred_element_type=F32)


def kernel(
    scale,
    feats_hbm,
    pos_hbm,
    phases_hbm,
    filt_hbm,
    w_hbm,
    tiles_smem,
    count_smem,
    out_ref,
    feats,
    pos,
    ph,
    ph2,
    filt,
    w,
    values,
    weight,
    req_pos,
    req_ids,
    in_pos,
    in_ids,
    columns,
    short,
    sh_send,
    sh_recv,
    rs_send,
    rs_recv,
    gat,
    l_own,
    l_send,
    l_recv,
    in_sem,
    rs_ssem,
    rs_rsem,
    ph_ssem,
    ph_rsem,
    rq_ssem,
    rq_rsem,
    sh_ssem,
    sh_rsem,
    ag_ssem,
    ag_rsem,
    sw_ssem,
    sw_rsem,
    l_ssem,
    l_rsem,
):
    a = lax.axis_index("atom")
    f = lax.axis_index("freq")
    core = lax.rem(a, 2)
    row = a // 2
    x_lo = row // 8
    z = lax.rem(row, 8)
    x_hi = f // 4
    y = lax.rem(f, 4)
    other = (1 - x_hi) * 4 + y

    def remote(src, dst, ssem, rsem, to):
        return pltpu.make_async_remote_copy(
            src_ref=src, dst_ref=dst, send_sem=ssem, recv_sem=rsem, device_id=to, device_id_type=MESH
        )

    step = 2048 // CHUNKS
    loads = [
        pltpu.make_async_copy(pos_hbm, pos, in_sem.at[0]),
        pltpu.make_async_copy(filt_hbm, filt, in_sem.at[1]),
        pltpu.make_async_copy(w_hbm, w, in_sem.at[2]),
    ]
    chunk_loads = []
    for i in range(CHUNKS):
        rows = pl.ds(i * step, step)
        trio = [
            pltpu.make_async_copy(phases_hbm.at[0, rows], ph.at[rows, pl.ds(0, 128)], in_sem.at[3 + 3 * i]),
            pltpu.make_async_copy(phases_hbm.at[1, rows], ph.at[rows, pl.ds(128, 128)], in_sem.at[4 + 3 * i]),
            pltpu.make_async_copy(feats_hbm.at[rows], feats.at[rows], in_sem.at[5 + 3 * i]),
        ]
        for c in trio:
            c.start()
        chunk_loads.append(trio)
    for c in loads:
        c.start()

    barrier = pltpu.get_barrier_semaphore()

    def greet(j, carry):
        pl.semaphore_signal(barrier, inc=1, device_id=(lax.rem(a + j, 32), f), device_id_type=MESH)
        return carry

    lax.fori_loop(1, 32, greet, 0)
    pl.semaphore_signal(barrier, inc=1, device_id=(a, other), device_id_type=MESH)
    for j in range(1, 4):
        pl.semaphore_signal(barrier, inc=1, device_id=(a, x_hi * 4 + lax.rem(y + j, 4)), device_id_type=MESH)

    total = None
    for i in range(CHUNKS):
        for c in chunk_loads[i]:
            c.wait()
        rows = pl.ds(i * step, step)
        part = lax.dot_general(
            ph[rows, :], feats[rows, :], (((0,), (0,)), ((), ())), preferred_element_type=F32
        )
        total = part if total is None else total + part
    for h in range(2):
        rs_send[h * 16 : (h + 1) * 16] = total[:, h * 128 : (h + 1) * 128].astype(BF16).reshape(16, 16, 128)

    loads[0].wait()
    req_pos[...] = jnp.zeros_like(req_pos)
    req_pos[0:3, :] = pos[:, pl.ds(pl.multiple_of(f * 256, 256), 256)]
    for t in range(2):
        for n in range(8):
            tile = jnp.where(n < count_smem[t], tiles_smem[t, n], -1)
            req_ids[t * 8 + n : t * 8 + n + 1, :] = jnp.full((1, 128), tile, jnp.int32)

    pl.semaphore_wait(barrier, 35)

    def send_part(j, carry):
        to = lax.rem(a + j, 32)
        remote(
            rs_send.at[lax.rem(to, 2) * 16 + to // 2], rs_recv.at[j], rs_ssem, rs_rsem, (to, f)
        ).start()
        return carry

    lax.fori_loop(1, 32, send_part, 0)
    before, after = lax.rem(a + 31, 32), lax.rem(a + 1, 32)
    asks = []
    for i, to in enumerate((before, after)):
        asks.append(remote(req_pos, in_pos.at[i], rq_ssem.at[2 * i], rq_rsem.at[2 * i], (to, f)))
        asks.append(remote(req_ids, in_ids.at[i], rq_ssem.at[2 * i + 1], rq_rsem.at[2 * i + 1], (to, f)))
    for c in asks:
        c.start()
    half = (1 - x_hi) * 1024
    early = remote(
        ph.at[pl.ds(half, FIRST)], ph2.at[pl.ds(0, FIRST)], ph_ssem.at[0], ph_rsem.at[0], (a, other)
    )
    late = remote(
        ph.at[pl.ds(half + FIRST, 1024 - FIRST)],
        ph2.at[pl.ds(FIRST, 1024 - FIRST)],
        ph_ssem.at[1],
        ph_rsem.at[1],
        (a, other),
    )
    early.start()

    loads[2].wait()
    for i in range(CHUNKS):
        rows = pl.ds(i * step, step)
        values[rows, :] = dot(feats[rows, :], w[...]).astype(BF16)

    def query(pos_ref, ids_ref):
        flipped = pos_ref[...].T
        for c in range(3):
            columns[c] = jnp.broadcast_to(flipped[:, c : c + 1], (256, 128))

        def tile(s, carry):
            lanes = pl.ds(pl.multiple_of(s * TILE, TILE), TILE)
            mine = a * 16 + s
            theirs = pos[:, lanes]
            for t in range(2):
                rows = pl.ds(t * TILE, TILE)
                live = jnp.max((ids_ref[t * 8 : (t + 1) * 8, :] == mine).astype(F32), axis=0, keepdims=True)
                dist = (1.0 - live) * FAR
                for c in range(3):
                    diff = columns[c, rows, :] - theirs[c : c + 1, :]
                    dist = dist + diff * diff
                weight[rows, lanes] = jnp.exp(-dist).astype(BF16)
            return carry

        lax.fori_loop(0, 16, tile, 0)
        return dot(weight[...], values[...])

    short[...] = query(req_pos, req_ids)

    parts = rs_recv.at[pl.ds(1, 31)]
    pltpu.make_async_copy(parts, parts, rs_rsem).wait()
    share = rs_send[core * 16 + row].astype(F32)
    share = share + jnp.sum(rs_recv[1:32].astype(F32), axis=0)
    loads[1].wait()
    k_rows = pl.ds(pl.multiple_of(lax.rem(row, 8) * 16, 16), 16)
    filt_share = jnp.where(core == 0, filt[k_rows, 0:128], filt[k_rows, 128:256])
    gat[core, row] = (filt_share * share * scale).astype(BF16)

    def send_share(k, carry):
        to = lax.rem((x_hi * 2 + x_lo) * 8 + z + k, 32)
        to_x, to_z = to // 8, lax.rem(to, 8)
        to_hi, to_lo = to_x // 2, lax.rem(to_x, 2)
        slot = lax.rem(to_hi + x_hi, 2) * 16 + row
        remote(
            gat.at[core, row],
            gat.at[core, slot],
            ag_ssem,
            ag_rsem,
            ((to_lo * 8 + to_z) * 2 + core, to_hi * 4 + y),
        ).start()
        return carry

    lax.fori_loop(1, 32, send_share, 0)
    late.start()

    answers = []
    for i, to in enumerate((before, after)):
        asks[2 * i].wait_recv()
        asks[2 * i + 1].wait_recv()
        sh_send[i] = query(in_pos.at[i], in_ids.at[i]).astype(BF16)
        answer = remote(
            sh_send.at[i], sh_recv.at[i], sh_ssem.at[i], sh_rsem.at[i], ((after, before)[i], f)
        )
        answer.start()
        answers.append(answer)

    shares = rs_recv.at[pl.ds(1, 31)]
    pltpu.make_async_copy(shares, shares, ag_rsem).wait()
    swap = remote(gat.at[core], gat.at[core], sw_ssem, sw_rsem, (row * 2 + 1 - core, f))
    swap.start()
    early.wait_recv()
    late.wait_recv()
    swap.wait_recv()

    mine = jnp.concatenate([gat[0, 0:16].reshape(256, 128), gat[1, 0:16].reshape(256, 128)], axis=1)
    twin = jnp.concatenate([gat[0, 16:32].reshape(256, 128), gat[1, 16:32].reshape(256, 128)], axis=1)

    def message(to):
        here = pl.ds(pl.multiple_of((x_hi * 4 + to) * 256, 256), 256)
        there = pl.ds(pl.multiple_of(to * 256, 256), 256)
        return dot(ph[here, :], mine) + dot(ph2[there, :], twin)

    sends = []
    for j in (2, 1, 3):
        to = lax.rem(y + j, 4)
        l_send[j - 1] = message(to).astype(BF16)
        c = remote(
            l_send.at[j - 1], l_recv.at[j - 1], l_ssem.at[j - 1], l_rsem.at[j - 1], (a, x_hi * 4 + to)
        )
        c.start()
        sends.append(c)
    l_own[...] = message(y)

    for c in answers:
        c.wait_recv()
    near = short[...] + sh_recv[0].astype(F32) + sh_recv[1].astype(F32)
    own = feats[pl.ds(pl.multiple_of(f * 256, 256), 256), :].astype(F32)
    l_own[...] = l_own[...] + near * (1.0 / math.sqrt(TILE)) + own
    for c in sends:
        c.wait_recv()
    far = l_recv[0].astype(F32) + l_recv[1].astype(F32) + l_recv[2].astype(F32)
    out_ref[...] = (l_own[...] + far).astype(BF16)

    pltpu.make_async_copy(parts, parts, rs_ssem).wait()
    pltpu.make_async_copy(parts, parts, ag_ssem).wait()
    for c in asks + answers + sends + [early, late, swap]:
        c.wait_send()


def shards(feats, positions, phases, filt, w_value, neighbour_tiles, neighbour_count):
    n_atom = lax.axis_size("atom")
    n_freq = lax.axis_size("freq")
    scale = 1.0 / math.sqrt(feats.shape[0] * n_atom * phases.shape[2] * n_freq)
    any_space = pl.BlockSpec(memory_space=pl.ANY)
    smem = pl.BlockSpec(memory_space=pltpu.SMEM)
    vmem, dma = pltpu.VMEM, pltpu.SemaphoreType.DMA
    return pl.pallas_call(
        functools.partial(kernel, scale),
        out_shape=jax.ShapeDtypeStruct((256, 256), BF16),
        in_specs=[any_space] * 5 + [smem] * 2,
        out_specs=pl.BlockSpec(memory_space=pltpu.VMEM),
        scratch_shapes=[
            vmem((2048, 256), BF16),
            vmem((3, 2048), F32),
            vmem((2048, 256), BF16),
            vmem((1024, 256), BF16),
            vmem((128, 256), F32),
            vmem((256, 256), BF16),
            vmem((2048, 256), BF16),
            vmem((256, 2048), BF16),
            vmem((8, 256), F32),
            vmem((16, 128), jnp.int32),
            vmem((2, 8, 256), F32),
            vmem((2, 16, 128), jnp.int32),
            vmem((3, 256, 128), F32),
            vmem((256, 256), F32),
            vmem((2, 256, 256), BF16),
            vmem((2, 256, 256), BF16),
            vmem((32, 16, 128), BF16),
            vmem((32, 16, 128), BF16),
            vmem((2, 32, 16, 128), BF16),
            vmem((256, 256), F32),
            vmem((3, 256, 256), BF16),
            vmem((3, 256, 256), BF16),
            dma((3 + 3 * CHUNKS,)),
            dma,
            dma,
            dma((2,)),
            dma((2,)),
            dma((4,)),
            dma((4,)),
            dma((2,)),
            dma((2,)),
            dma,
            dma,
            dma,
            dma,
            dma((3,)),
            dma((3,)),
        ],
        compiler_params=pltpu.CompilerParams(
            collective_id=0, has_side_effects=True, vmem_limit_bytes=66_000_000
        ),
    )(feats, positions, phases, filt, w_value, neighbour_tiles, neighbour_count)


def solution(mesh):
    in_specs = (
        P("atom", None),
        P(None, "atom"),
        P(None, "atom", "freq"),
        P("freq", None),
        P(),
        P(("atom", "freq"), None),
        P(("atom", "freq")),
    )
    out_specs = P(("atom", "freq"), None)
    return jax.shard_map(shards, mesh=mesh, in_specs=in_specs, out_specs=out_specs, check_vma=False)
```

time: 75 us -> 42.1 us (0.56)
  the two profiles are of different devices: /device:TPU:8 before, /device:TPU:1 now
where the time goes in v1:
time: 42.1 us; the launch traced here: 41.9 us
  Pallas kernels  40.4 us (96%)
  local copies, waits for them, and re-layouts  1.57 us (4%)
    pallas_call x1, Pallas kernels, shards(): pl.pallas_call(functools.partial(kernel, scale), out_shape=jax.ShapeDtype...  40.4 us
    unnamed x1, local copies, waits for them, and re-layouts  1.57 us

profile of v1, /device:TPU:1, one launch (start us, length us, event | category | flops | bytes accessed | tf_op | source)
XLA Modules:
  0.0 41.9 jit_solution(2794151513532649315)
XLA Ops:
  0.0 40.4 %shard_map.73 = bf16[256,256]{1,0:T(8,128)(2,1)} custom-call(bf16[2048,256]{1,0:T(8,128)(2,1)} %feats_hbm.1, f32[3,2048]{1,0:T(4,128)} %pos_hbm.1, bf16[2,2048,128]{2,1,0:T(8,128)(2,1)} %phases_hbm.1, f32[128,256]{1,0:T(8,128)} %filt_hbm.1, bf16[256,256]{1,0:T(8,128)(2,1)} %w_hbm.1, s32[2,8]{1,0:T(2,128)} %tiles_smem.1, s32[2]{0:T(128)} %count_smem.1), custom_call_target="tpu_custom_call" | custom-call | tf_op jit(solution)/shard_map/pallas_call | solution.py:285
  40.4 1.6 %copy.9 = bf16[256,256]{1,0:T(8,128)(2,1)} copy(bf16[256,256]{1,0:T(8,128)(2,1)} %shard_map.73) | data formatting | bytes 262144

commit v2 on v1

--- a/solution.py
+++ b/solution.py
@@ -10,8 +10,7 @@
 
 MESH = pl.DeviceIdType.MESH
 TILE = 128
-CHUNKS = 4
-FIRST = 448
+CHUNKS = 2
 FAR = 1e30
 
 F32 = jnp.float32
@@ -35,7 +34,7 @@
     feats,
     pos,
     ph,
-    ph2,
+    lent,
     filt,
     w,
     values,
@@ -63,8 +62,10 @@
     rq_rsem,
     sh_ssem,
     sh_rsem,
-    ag_ssem,
-    ag_rsem,
+    az_ssem,
+    az_rsem,
+    ap_ssem,
+    ap_rsem,
     sw_ssem,
     sw_rsem,
     l_ssem,
@@ -153,18 +154,18 @@
         asks.append(remote(req_ids, in_ids.at[i], rq_ssem.at[2 * i + 1], rq_rsem.at[2 * i + 1], (to, f)))
     for c in asks:
         c.start()
-    half = (1 - x_hi) * 1024
-    early = remote(
-        ph.at[pl.ds(half, FIRST)], ph2.at[pl.ds(0, FIRST)], ph_ssem.at[0], ph_rsem.at[0], (a, other)
-    )
-    late = remote(
-        ph.at[pl.ds(half + FIRST, 1024 - FIRST)],
-        ph2.at[pl.ds(FIRST, 1024 - FIRST)],
-        ph_ssem.at[1],
-        ph_rsem.at[1],
-        (a, other),
-    )
-    early.start()
+
+    def lend(j, hi):
+        to = lax.rem(y + j, 4)
+        rows = pl.ds(pl.multiple_of((lax.rem(x_hi + hi, 2) * 4 + to) * 256, 256), 256)
+        i = (j - 1) * 2 + hi
+        return remote(
+            ph.at[rows], lent.at[j - 1, hi], ph_ssem.at[i], ph_rsem.at[i], (a, x_hi * 4 + to)
+        )
+
+    loans = {(j, hi): lend(j, hi) for hi in (1, 0) for j in (1, 3, 2)}
+    for key in ((1, 1), (3, 1), (2, 1), (1, 0), (3, 0)):
+        loans[key].start()
 
     loads[2].wait()
     for i in range(CHUNKS):
@@ -202,62 +203,66 @@
     loads[1].wait()
     k_rows = pl.ds(pl.multiple_of(lax.rem(row, 8) * 16, 16), 16)
     filt_share = jnp.where(core == 0, filt[k_rows, 0:128], filt[k_rows, 128:256])
-    gat[core, row] = (filt_share * share * scale).astype(BF16)
-
-    def send_share(k, carry):
-        to = lax.rem((x_hi * 2 + x_lo) * 8 + z + k, 32)
-        to_x, to_z = to // 8, lax.rem(to, 8)
-        to_hi, to_lo = to_x // 2, lax.rem(to_x, 2)
-        slot = lax.rem(to_hi + x_hi, 2) * 16 + row
-        remote(
-            gat.at[core, row],
-            gat.at[core, slot],
-            ag_ssem,
-            ag_rsem,
-            ((to_lo * 8 + to_z) * 2 + core, to_hi * 4 + y),
-        ).start()
-        return carry
-
-    lax.fori_loop(1, 32, send_share, 0)
-    late.start()
+    gat[core, 0, x_lo, z] = (filt_share * share * scale).astype(BF16)
+
+    along_z = []
+    for j in (4, 3, 5, 2, 6, 1, 7):
+        to = (x_lo * 8 + lax.rem(z + j, 8)) * 2 + core
+        mine = gat.at[core, 0, x_lo, z]
+        along_z.append(remote(mine, mine, az_ssem, az_rsem, (to, f)))
+        along_z[-1].start()
 
     answers = []
-    for i, to in enumerate((before, after)):
+
+    def answer(i, to):
         asks[2 * i].wait_recv()
         asks[2 * i + 1].wait_recv()
         sh_send[i] = query(in_pos.at[i], in_ids.at[i]).astype(BF16)
-        answer = remote(
-            sh_send.at[i], sh_recv.at[i], sh_ssem.at[i], sh_rsem.at[i], ((after, before)[i], f)
+        answers.append(remote(sh_send.at[i], sh_recv.at[i], sh_ssem.at[i], sh_rsem.at[i], (to, f)))
+        answers[-1].start()
+
+    answer(0, after)
+    seven = gat.at[0, 0, 0, pl.ds(0, 7)]
+    pltpu.make_async_copy(seven, seven, az_rsem).wait()
+    plane = []
+    for j, flip in ((2, 1), (2, 0), (1, 1), (3, 1), (1, 0), (3, 0), (0, 1)):
+        to = ((lax.rem(x_lo + flip, 2) * 8 + z) * 2 + core, x_hi * 4 + lax.rem(y + j, 4))
+        plane.append(
+            remote(gat.at[core, 0, x_lo], gat.at[core, (4 - j) % 4, x_lo], ap_ssem, ap_rsem, to)
         )
-        answer.start()
-        answers.append(answer)
-
-    shares = rs_recv.at[pl.ds(1, 31)]
-    pltpu.make_async_copy(shares, shares, ag_rsem).wait()
+        plane[-1].start()
+    loans[2, 0].start()
+    seven_rows = feats.at[pl.ds(0, 7 * 64)]
+    answer(1, before)
+    pltpu.make_async_copy(seven_rows, seven_rows, ap_rsem).wait()
     swap = remote(gat.at[core], gat.at[core], sw_ssem, sw_rsem, (row * 2 + 1 - core, f))
     swap.start()
-    early.wait_recv()
-    late.wait_recv()
-    swap.wait_recv()
-
-    mine = jnp.concatenate([gat[0, 0:16].reshape(256, 128), gat[1, 0:16].reshape(256, 128)], axis=1)
-    twin = jnp.concatenate([gat[0, 16:32].reshape(256, 128), gat[1, 16:32].reshape(256, 128)], axis=1)
-
-    def message(to):
-        here = pl.ds(pl.multiple_of((x_hi * 4 + to) * 256, 256), 256)
-        there = pl.ds(pl.multiple_of(to * 256, 256), 256)
-        return dot(ph[here, :], mine) + dot(ph2[there, :], twin)
-
+
+    def message(hi, filtered):
+        rows = pl.ds(pl.multiple_of((lax.rem(x_hi + hi, 2) * 4 + y) * 256, 256), 256)
+        out = dot(ph[rows, :], filtered(0))
+        for j in range(1, 4):
+            out = out + dot(lent[j - 1, hi], filtered(4 - j))
+        return out
+
+    def half(h):
+        return lambda j: gat[h, j].reshape(256, 128)
+
+    def whole(j):
+        return jnp.concatenate([gat[0, j].reshape(256, 128), gat[1, j].reshape(256, 128)], axis=1)
+
+    for j in (1, 3, 2):
+        loans[j, 1].wait_recv()
     sends = []
-    for j in (2, 1, 3):
-        to = lax.rem(y + j, 4)
-        l_send[j - 1] = message(to).astype(BF16)
-        c = remote(
-            l_send.at[j - 1], l_recv.at[j - 1], l_ssem.at[j - 1], l_rsem.at[j - 1], (a, x_hi * 4 + to)
-        )
-        c.start()
-        sends.append(c)
-    l_own[...] = message(y)
+    for i, h in enumerate((core, 1 - core)):
+        if i == 1:
+            swap.wait_recv()
+        l_send[h] = message(1, half(h)).astype(BF16)
+        sends.append(remote(l_send.at[h], l_recv.at[h], l_ssem.at[i], l_rsem.at[i], (a, other)))
+        sends[-1].start()
+    for j in (1, 3, 2):
+        loans[j, 0].wait_recv()
+    l_own[...] = message(0, whole)
 
     for c in answers:
         c.wait_recv()
@@ -266,12 +271,13 @@
     l_own[...] = l_own[...] + near * (1.0 / math.sqrt(TILE)) + own
     for c in sends:
         c.wait_recv()
-    far = l_recv[0].astype(F32) + l_recv[1].astype(F32) + l_recv[2].astype(F32)
+    far = jnp.concatenate([l_recv[0].astype(F32), l_recv[1].astype(F32)], axis=1)
     out_ref[...] = (l_own[...] + far).astype(BF16)
 
     pltpu.make_async_copy(parts, parts, rs_ssem).wait()
-    pltpu.make_async_copy(parts, parts, ag_ssem).wait()
-    for c in asks + answers + sends + [early, late, swap]:
+    pltpu.make_async_copy(seven, seven, az_ssem).wait()
+    pltpu.make_async_copy(seven_rows, seven_rows, ap_ssem).wait()
+    for c in asks + answers + sends + [swap] + list(loans.values()):
         c.wait_send()
 
 
@@ -291,7 +297,7 @@
             vmem((2048, 256), BF16),
             vmem((3, 2048), F32),
             vmem((2048, 256), BF16),
-            vmem((1024, 256), BF16),
+            vmem((3, 2, 256, 256), BF16),
             vmem((128, 256), F32),
             vmem((256, 256), BF16),
             vmem((2048, 256), BF16),
@@ -306,15 +312,15 @@
             vmem((2, 256, 256), BF16),
             vmem((32, 16, 128), BF16),
             vmem((32, 16, 128), BF16),
-            vmem((2, 32, 16, 128), BF16),
+            vmem((2, 4, 2, 8, 16, 128), BF16),
             vmem((256, 256), F32),
-            vmem((3, 256, 256), BF16),
-            vmem((3, 256, 256), BF16),
+            vmem((2, 256, 128), BF16),
+            vmem((2, 256, 128), BF16),
             dma((3 + 3 * CHUNKS,)),
             dma,
             dma,
-            dma((2,)),
-            dma((2,)),
+            dma((6,)),
+            dma((6,)),
             dma((4,)),
             dma((4,)),
             dma((2,)),
@@ -323,8 +329,10 @@
             dma,
             dma,
             dma,
-            dma((3,)),
-            dma((3,)),
+            dma,
+            dma,
+            dma((2,)),
+            dma((2,)),
         ],
         compiler_params=pltpu.CompilerParams(
             collective_id=0, has_side_effects=True, vmem_limit_bytes=66_000_000

time: 42.1 us -> 38.1 us (0.905)
  Pallas kernels: 40.4 us -> 36.4 us
    pallas_call x1, Pallas kernels: 40.4 us -> 36.4 us  [shards(): pl.pallas_call(functools.partial(kernel, scale), out_shape=jax.ShapeDtype...]
where the time goes in v2:
time: 38.1 us; the launch traced here: 37.9 us
  Pallas kernels  36.4 us (96%)
  local copies, waits for them, and re-layouts  1.57 us (4%)
    pallas_call x1, Pallas kernels, shards(): pl.pallas_call(functools.partial(kernel, scale), out_shape=jax.ShapeDtype...  36.4 us
    unnamed x1, local copies, waits for them, and re-layouts  1.57 us

profile of v2, /device:TPU:1, one launch (start us, length us, event | category | flops | bytes accessed | tf_op | source)
XLA Modules:
  0.0 37.9 jit_solution(2519006790994875935)
XLA Ops:
  0.0 36.4 %shard_map.73 = bf16[256,256]{1,0:T(8,128)(2,1)} custom-call(bf16[2048,256]{1,0:T(8,128)(2,1)} %feats_hbm.1, f32[3,2048]{1,0:T(4,128)} %pos_hbm.1, bf16[2,2048,128]{2,1,0:T(8,128)(2,1)} %phases_hbm.1, f32[128,256]{1,0:T(8,128)} %filt_hbm.1, bf16[256,256]{1,0:T(8,128)(2,1)} %w_hbm.1, s32[2,8]{1,0:T(2,128)} %tiles_smem.1, s32[2]{0:T(128)} %count_smem.1), custom_call_target="tpu_custom_call" | custom-call | tf_op jit(solution)/shard_map/pallas_call | solution.py:291
  36.4 1.6 %copy.9 = bf16[256,256]{1,0:T(8,128)(2,1)} copy(bf16[256,256]{1,0:T(8,128)(2,1)} %shard_map.73) | data formatting | bytes 262144

commit v3 on v2

--- a/solution.py
+++ b/solution.py
@@ -12,6 +12,7 @@
 TILE = 128
 CHUNKS = 2
 FAR = 1e30
+ATOM_PEERS = [(i, j, k) for j in (4, 3, 5, 2, 6, 1, 7, 0) for i in (1, 0) for k in (1, 0) if i + j + k > 0]
 
 F32 = jnp.float32
 BF16 = jnp.bfloat16
@@ -28,9 +29,11 @@
     phases_hbm,
     filt_hbm,
     w_hbm,
+    tiles_hbm,
+    count_hbm,
+    out_ref,
     tiles_smem,
     count_smem,
-    out_ref,
     feats,
     pos,
     ph,
@@ -86,36 +89,45 @@
             src_ref=src, dst_ref=dst, send_sem=ssem, recv_sem=rsem, device_id=to, device_id_type=MESH
         )
 
+    z_at = [lax.rem(z + j, 8) * 2 for j in range(8)]
+    x_at = [x_lo * 16, (1 - x_lo) * 16]
+    core_at = [core, 1 - core]
+
+    def block_at(d):
+        return x_at[d[0]] + z_at[d[1]] + core_at[d[2]]
+
+    barrier = pltpu.get_barrier_semaphore()
+
+    def greet(to):
+        pl.semaphore_signal(barrier, inc=1, device_id=to, device_id_type=MESH)
+
+    for d in ATOM_PEERS:
+        greet((block_at(d), f))
+    for j in (2, 1, 3):
+        greet((a, x_hi * 4 + lax.rem(y + j, 4)))
+    greet((a, other))
+
     step = 2048 // CHUNKS
     loads = [
         pltpu.make_async_copy(pos_hbm, pos, in_sem.at[0]),
         pltpu.make_async_copy(filt_hbm, filt, in_sem.at[1]),
         pltpu.make_async_copy(w_hbm, w, in_sem.at[2]),
+        pltpu.make_async_copy(tiles_hbm, tiles_smem, in_sem.at[3]),
+        pltpu.make_async_copy(count_hbm, count_smem, in_sem.at[4]),
     ]
     chunk_loads = []
     for i in range(CHUNKS):
         rows = pl.ds(i * step, step)
         trio = [
-            pltpu.make_async_copy(phases_hbm.at[0, rows], ph.at[rows, pl.ds(0, 128)], in_sem.at[3 + 3 * i]),
-            pltpu.make_async_copy(phases_hbm.at[1, rows], ph.at[rows, pl.ds(128, 128)], in_sem.at[4 + 3 * i]),
-            pltpu.make_async_copy(feats_hbm.at[rows], feats.at[rows], in_sem.at[5 + 3 * i]),
+            pltpu.make_async_copy(phases_hbm.at[0, rows], ph.at[rows, pl.ds(0, 128)], in_sem.at[5 + 3 * i]),
+            pltpu.make_async_copy(phases_hbm.at[1, rows], ph.at[rows, pl.ds(128, 128)], in_sem.at[6 + 3 * i]),
+            pltpu.make_async_copy(feats_hbm.at[rows], feats.at[rows], in_sem.at[7 + 3 * i]),
         ]
         for c in trio:
             c.start()
         chunk_loads.append(trio)
     for c in loads:
         c.start()
-
-    barrier = pltpu.get_barrier_semaphore()
-
-    def greet(j, carry):
-        pl.semaphore_signal(barrier, inc=1, device_id=(lax.rem(a + j, 32), f), device_id_type=MESH)
-        return carry
-
-    lax.fori_loop(1, 32, greet, 0)
-    pl.semaphore_signal(barrier, inc=1, device_id=(a, other), device_id_type=MESH)
-    for j in range(1, 4):
-        pl.semaphore_signal(barrier, inc=1, device_id=(a, x_hi * 4 + lax.rem(y + j, 4)), device_id_type=MESH)
 
     total = None
     for i in range(CHUNKS):
@@ -130,6 +142,8 @@
         rs_send[h * 16 : (h + 1) * 16] = total[:, h * 128 : (h + 1) * 128].astype(BF16).reshape(16, 16, 128)
 
     loads[0].wait()
+    loads[3].wait()
+    loads[4].wait()
     req_pos[...] = jnp.zeros_like(req_pos)
     req_pos[0:3, :] = pos[:, pl.ds(pl.multiple_of(f * 256, 256), 256)]
     for t in range(2):
@@ -139,14 +153,10 @@
 
     pl.semaphore_wait(barrier, 35)
 
-    def send_part(j, carry):
-        to = lax.rem(a + j, 32)
-        remote(
-            rs_send.at[lax.rem(to, 2) * 16 + to // 2], rs_recv.at[j], rs_ssem, rs_rsem, (to, f)
-        ).start()
-        return carry
-
-    lax.fori_loop(1, 32, send_part, 0)
+    for i, d in enumerate(ATOM_PEERS):
+        to = block_at(d)
+        share_of = core_at[d[2]] * 16 + (x_at[d[0]] + z_at[d[1]]) // 2
+        remote(rs_send.at[share_of], rs_recv.at[i + 1], rs_ssem, rs_rsem, (to, f)).start()
     before, after = lax.rem(a + 31, 32), lax.rem(a + 1, 32)
     asks = []
     for i, to in enumerate((before, after)):
@@ -285,15 +295,20 @@
     n_atom = lax.axis_size("atom")
     n_freq = lax.axis_size("freq")
     scale = 1.0 / math.sqrt(feats.shape[0] * n_atom * phases.shape[2] * n_freq)
-    any_space = pl.BlockSpec(memory_space=pl.ANY)
-    smem = pl.BlockSpec(memory_space=pltpu.SMEM)
+    in_hbm = pl.BlockSpec(memory_space=pltpu.HBM)
     vmem, dma = pltpu.VMEM, pltpu.SemaphoreType.DMA
+    operands = [
+        pltpu.with_memory_space_constraint(x, pltpu.HBM)
+        for x in (feats, positions, phases, filt, w_value, neighbour_tiles, neighbour_count)
+    ]
     return pl.pallas_call(
         functools.partial(kernel, scale),
         out_shape=jax.ShapeDtypeStruct((256, 256), BF16),
-        in_specs=[any_space] * 5 + [smem] * 2,
+        in_specs=[in_hbm] * 7,
         out_specs=pl.BlockSpec(memory_space=pltpu.VMEM),
         scratch_shapes=[
+            pltpu.SMEM((2, 8), jnp.int32),
+            pltpu.SMEM((2,), jnp.int32),
             vmem((2048, 256), BF16),
             vmem((3, 2048), F32),
             vmem((2048, 256), BF16),
@@ -316,7 +331,7 @@
             vmem((256, 256), F32),
             vmem((2, 256, 128), BF16),
             vmem((2, 256, 128), BF16),
-            dma((3 + 3 * CHUNKS,)),
+            dma((5 + 3 * CHUNKS,)),
             dma,
             dma,
             dma((6,)),
@@ -335,9 +350,9 @@
             dma((2,)),
         ],
         compiler_params=pltpu.CompilerParams(
-            collective_id=0, has_side_effects=True, vmem_limit_bytes=66_000_000
+            collective_id=0, has_side_effects=True, vmem_limit_bytes=40_000_000
         ),
-    )(feats, positions, phases, filt, w_value, neighbour_tiles, neighbour_count)
+    )(*operands)
 
 
 def solution(mesh):

time: 38.1 us -> 34.8 us (0.913)
  Pallas kernels: 36.4 us -> 34.1 us
  local copies, waits for them, and re-layouts: 1.57 us -> 0.66 us
    pallas_call x1, Pallas kernels: 36.4 us -> 34.1 us  [shards(): pl.pallas_call(functools.partial(kernel, scale), out_shape=jax.ShapeDtype...]
    unnamed x1, local copies, waits for them, and re-layouts: 1.57 us -> 0.66 us
where the time goes in v3:
time: 34.8 us; the launch traced here: 34.7 us
  Pallas kernels  34.1 us (98%)
  local copies, waits for them, and re-layouts  0.66 us (2%)
    pallas_call x1, Pallas kernels, shards(): pl.pallas_call(functools.partial(kernel, scale), out_shape=jax.ShapeDtype...  34.1 us

profile of v3, /device:TPU:1, one launch (start us, length us, event | category | flops | bytes accessed | tf_op | source)
XLA Modules:
  0.0 34.7 jit_solution(9769983296251300288)
XLA Ops:
  0.0 34.1 %shard_map.73 = bf16[256,256]{1,0:T(8,128)(2,1)S(1)} custom-call(bf16[2048,256]{1,0:T(8,128)(2,1)} %feats_hbm.1, f32[3,2048]{1,0:T(4,128)} %pos_hbm.1, bf16[2,2048,128]{2,1,0:T(8,128)(2,1)} %phases_hbm.1, f32[128,256]{1,0:T(8,128)} %filt_hbm.1, bf16[256,256]{1,0:T(8,128)(2,1)} %w_hbm.1, s32[2,8]{1,0:T(2,128)} %tiles_hbm.1, s32[2]{0:T(128)} %count_hbm.1), custom_call_target="tpu_custom_call" | custom-call | tf_op jit(solution)/shard_map/pallas_call | solution.py:304
  34.1 0.7 %copy.9 = bf16[256,256]{1,0:T(8,128)(2,1)} copy(bf16[256,256]{1,0:T(8,128)(2,1)S(1)} %shard_map.73) | data formatting | bytes 262144

commit v4 on v3

--- a/solution.py
+++ b/solution.py
@@ -12,6 +12,7 @@
 TILE = 128
 CHUNKS = 2
 FAR = 1e30
+LATE = ((2, 0),)
 ATOM_PEERS = [(i, j, k) for j in (4, 3, 5, 2, 6, 1, 7, 0) for i in (1, 0) for k in (1, 0) if i + j + k > 0]
 
 F32 = jnp.float32
@@ -174,8 +175,9 @@
         )
 
     loans = {(j, hi): lend(j, hi) for hi in (1, 0) for j in (1, 3, 2)}
-    for key in ((1, 1), (3, 1), (2, 1), (1, 0), (3, 0)):
-        loans[key].start()
+    for key in loans:
+        if key not in LATE:
+            loans[key].start()
 
     loads[2].wait()
     for i in range(CHUNKS):
@@ -215,12 +217,10 @@
     filt_share = jnp.where(core == 0, filt[k_rows, 0:128], filt[k_rows, 128:256])
     gat[core, 0, x_lo, z] = (filt_share * share * scale).astype(BF16)
 
-    along_z = []
-    for j in (4, 3, 5, 2, 6, 1, 7):
-        to = (x_lo * 8 + lax.rem(z + j, 8)) * 2 + core
-        mine = gat.at[core, 0, x_lo, z]
-        along_z.append(remote(mine, mine, az_ssem, az_rsem, (to, f)))
-        along_z[-1].start()
+    mine = gat.at[core, 0, x_lo, z]
+    for d in ATOM_PEERS:
+        if d[2] == 0:
+            remote(mine, mine, az_ssem, az_rsem, (block_at(d), f)).start()
 
     answers = []
 
@@ -229,50 +229,58 @@
         asks[2 * i + 1].wait_recv()
         sh_send[i] = query(in_pos.at[i], in_ids.at[i]).astype(BF16)
         answers.append(remote(sh_send.at[i], sh_recv.at[i], sh_ssem.at[i], sh_rsem.at[i], (to, f)))
-        answers[-1].start()
 
     answer(0, after)
-    seven = gat.at[0, 0, 0, pl.ds(0, 7)]
-    pltpu.make_async_copy(seven, seven, az_rsem).wait()
+    fifteen = rs_recv.at[pl.ds(1, 15)]
+    pltpu.make_async_copy(fifteen, fifteen, az_rsem).wait()
     plane = []
-    for j, flip in ((2, 1), (2, 0), (1, 1), (3, 1), (1, 0), (3, 0), (0, 1)):
-        to = ((lax.rem(x_lo + flip, 2) * 8 + z) * 2 + core, x_hi * 4 + lax.rem(y + j, 4))
-        plane.append(
-            remote(gat.at[core, 0, x_lo], gat.at[core, (4 - j) % 4, x_lo], ap_ssem, ap_rsem, to)
-        )
+    for j in (2, 1, 3):
+        to = (a, x_hi * 4 + lax.rem(y + j, 4))
+        plane.append(remote(gat.at[core, 0], gat.at[core, 4 - j], ap_ssem.at[j - 1], ap_rsem.at[j - 1], to))
         plane[-1].start()
-    loans[2, 0].start()
-    seven_rows = feats.at[pl.ds(0, 7 * 64)]
+    answers[0].start()
     answer(1, before)
-    pltpu.make_async_copy(seven_rows, seven_rows, ap_rsem).wait()
-    swap = remote(gat.at[core], gat.at[core], sw_ssem, sw_rsem, (row * 2 + 1 - core, f))
-    swap.start()
-
-    def message(hi, filtered):
-        rows = pl.ds(pl.multiple_of((lax.rem(x_hi + hi, 2) * 4 + y) * 256, 256), 256)
-        out = dot(ph[rows, :], filtered(0))
-        for j in range(1, 4):
-            out = out + dot(lent[j - 1, hi], filtered(4 - j))
-        return out
-
-    def half(h):
-        return lambda j: gat[h, j].reshape(256, 128)
-
-    def whole(j):
-        return jnp.concatenate([gat[0, j].reshape(256, 128), gat[1, j].reshape(256, 128)], axis=1)
+    answers[1].start()
+    for key in LATE:
+        loans[key].start()
+
+    def term(hi, s, filtered):
+        if s == 0:
+            rows = pl.ds(pl.multiple_of((lax.rem(x_hi + hi, 2) * 4 + y) * 256, 256), 256)
+            return dot(ph[rows, :], filtered)
+        return dot(lent[3 - s, hi], filtered)
 
     for j in (1, 3, 2):
         loans[j, 1].wait_recv()
-    sends = []
-    for i, h in enumerate((core, 1 - core)):
-        if i == 1:
-            swap.wait_recv()
-        l_send[h] = message(1, half(h)).astype(BF16)
-        sends.append(remote(l_send.at[h], l_recv.at[h], l_ssem.at[i], l_rsem.at[i], (a, other)))
-        sends[-1].start()
-    for j in (1, 3, 2):
-        loans[j, 0].wait_recv()
-    l_own[...] = message(0, whole)
+    swaps = []
+    first = None
+    for s in (0, 1, 3, 2):
+        if s:
+            plane[(2, 1, 3).index(4 - s)].wait_recv()
+        swaps.append(remote(gat.at[core, s], gat.at[core, s], sw_ssem.at[s], sw_rsem.at[s], (row * 2 + 1 - core, f)))
+        swaps[-1].start()
+        part = term(1, s, gat[core, s].reshape(256, 128))
+        first = part if first is None else first + part
+    l_send[core] = first.astype(BF16)
+    sends = [remote(l_send.at[core], l_recv.at[core], l_ssem.at[0], l_rsem.at[0], (a, other))]
+    sends[0].start()
+    second = None
+    for s, swap in zip((0, 1, 3, 2), swaps):
+        swap.wait_recv()
+        part = term(1, s, gat[1 - core, s].reshape(256, 128))
+        second = part if second is None else second + part
+    l_send[1 - core] = second.astype(BF16)
+    sends.append(remote(l_send.at[1 - core], l_recv.at[1 - core], l_ssem.at[1], l_rsem.at[1], (a, other)))
+    sends[1].start()
+
+    mine = None
+    for s in (0, 1, 3, 2):
+        if s:
+            loans[4 - s, 0].wait_recv()
+        both = jnp.concatenate([gat[0, s].reshape(256, 128), gat[1, s].reshape(256, 128)], axis=1)
+        part = term(0, s, both)
+        mine = part if mine is None else mine + part
+    l_own[...] = mine
 
     for c in answers:
         c.wait_recv()
@@ -285,9 +293,8 @@
     out_ref[...] = (l_own[...] + far).astype(BF16)
 
     pltpu.make_async_copy(parts, parts, rs_ssem).wait()
-    pltpu.make_async_copy(seven, seven, az_ssem).wait()
-    pltpu.make_async_copy(seven_rows, seven_rows, ap_ssem).wait()
-    for c in asks + answers + sends + [swap] + list(loans.values()):
+    pltpu.make_async_copy(fifteen, fifteen, az_ssem).wait()
+    for c in asks + plane + answers + sends + swaps + list(loans.values()):
         c.wait_send()
 
 
@@ -342,10 +349,10 @@
             dma((2,)),
             dma,
             dma,
-            dma,
-            dma,
-            dma,
-            dma,
+            dma((3,)),
+            dma((3,)),
+            dma((4,)),
+            dma((4,)),
             dma((2,)),
             dma((2,)),
         ],

time: 34.8 us -> 34.7 us (level)
  no operation moved by 1% of the time
where the time goes in v4:
time: 34.7 us; the launch traced here: 34.6 us
  Pallas kernels  33.9 us (98%)
  local copies, waits for them, and re-layouts  0.66 us (2%)
    pallas_call x1, Pallas kernels, shards(): pl.pallas_call(functools.partial(kernel, scale), out_shape=jax.ShapeDtype...  33.9 us

profile of v4, /device:TPU:1, one launch (start us, length us, event | category | flops | bytes accessed | tf_op | source)
XLA Modules:
  0.0 34.6 jit_solution(10023507507713046141)
XLA Ops:
  0.0 33.9 %shard_map.73 = bf16[256,256]{1,0:T(8,128)(2,1)S(1)} custom-call(bf16[2048,256]{1,0:T(8,128)(2,1)} %feats_hbm.1, f32[3,2048]{1,0:T(4,128)} %pos_hbm.1, bf16[2,2048,128]{2,1,0:T(8,128)(2,1)} %phases_hbm.1, f32[128,256]{1,0:T(8,128)} %filt_hbm.1, bf16[256,256]{1,0:T(8,128)(2,1)} %w_hbm.1, s32[2,8]{1,0:T(2,128)} %tiles_hbm.1, s32[2]{0:T(128)} %count_hbm.1), custom_call_target="tpu_custom_call" | custom-call | tf_op jit(solution)/shard_map/pallas_call | solution.py:311
  33.9 0.7 %copy.9 = bf16[256,256]{1,0:T(8,128)(2,1)} copy(bf16[256,256]{1,0:T(8,128)(2,1)S(1)} %shard_map.73) | data formatting | bytes 262144

commit v5 on v4

--- a/solution.py
+++ b/solution.py
@@ -12,7 +12,7 @@
 TILE = 128
 CHUNKS = 2
 FAR = 1e30
-LATE = ((2, 0),)
+LATE = ((2, 1), (1, 0), (3, 0), (2, 0))
 ATOM_PEERS = [(i, j, k) for j in (4, 3, 5, 2, 6, 1, 7, 0) for i in (1, 0) for k in (1, 0) if i + j + k > 0]
 
 F32 = jnp.float32
@@ -66,8 +66,6 @@
     rq_rsem,
     sh_ssem,
     sh_rsem,
-    az_ssem,
-    az_rsem,
     ap_ssem,
     ap_rsem,
     sw_ssem,
@@ -217,10 +215,22 @@
     filt_share = jnp.where(core == 0, filt[k_rows, 0:128], filt[k_rows, 128:256])
     gat[core, 0, x_lo, z] = (filt_share * share * scale).astype(BF16)
 
-    mine = gat.at[core, 0, x_lo, z]
-    for d in ATOM_PEERS:
-        if d[2] == 0:
-            remote(mine, mine, az_ssem, az_rsem, (block_at(d), f)).start()
+    y_at = [x_hi * 4 + lax.rem(y + j, 4) for j in range(4)]
+    for dz in (4, 3, 5, 2, 6, 1, 7, 0):
+        for j in (2, 1, 3, 0):
+            for i in (1, 0):
+                if dz + j + i > 0:
+                    slot = (4 - j) % 4
+                    remote(
+                        gat.at[core, 0, x_lo, z],
+                        gat.at[core, slot, x_lo, z],
+                        ap_ssem.at[slot],
+                        ap_rsem.at[slot],
+                        (x_at[i] + z_at[dz] + core, y_at[j]),
+                    ).start()
+
+    for key in LATE:
+        loans[key].start()
 
     answers = []
 
@@ -231,18 +241,7 @@
         answers.append(remote(sh_send.at[i], sh_recv.at[i], sh_ssem.at[i], sh_rsem.at[i], (to, f)))
 
     answer(0, after)
-    fifteen = rs_recv.at[pl.ds(1, 15)]
-    pltpu.make_async_copy(fifteen, fifteen, az_rsem).wait()
-    plane = []
-    for j in (2, 1, 3):
-        to = (a, x_hi * 4 + lax.rem(y + j, 4))
-        plane.append(remote(gat.at[core, 0], gat.at[core, 4 - j], ap_ssem.at[j - 1], ap_rsem.at[j - 1], to))
-        plane[-1].start()
-    answers[0].start()
     answer(1, before)
-    answers[1].start()
-    for key in LATE:
-        loans[key].start()
 
     def term(hi, s, filtered):
         if s == 0:
@@ -255,8 +254,8 @@
     swaps = []
     first = None
     for s in (0, 1, 3, 2):
-        if s:
-            plane[(2, 1, 3).index(4 - s)].wait_recv()
+        arrived = rs_recv.at[pl.ds(1, 16 if s else 15)]
+        pltpu.make_async_copy(arrived, arrived, ap_rsem.at[s]).wait()
         swaps.append(remote(gat.at[core, s], gat.at[core, s], sw_ssem.at[s], sw_rsem.at[s], (row * 2 + 1 - core, f)))
         swaps[-1].start()
         part = term(1, s, gat[core, s].reshape(256, 128))
@@ -264,6 +263,8 @@
     l_send[core] = first.astype(BF16)
     sends = [remote(l_send.at[core], l_recv.at[core], l_ssem.at[0], l_rsem.at[0], (a, other))]
     sends[0].start()
+    for c in answers:
+        c.start()
     second = None
     for s, swap in zip((0, 1, 3, 2), swaps):
         swap.wait_recv()
@@ -293,8 +294,10 @@
     out_ref[...] = (l_own[...] + far).astype(BF16)
 
     pltpu.make_async_copy(parts, parts, rs_ssem).wait()
-    pltpu.make_async_copy(fifteen, fifteen, az_ssem).wait()
-    for c in asks + plane + answers + sends + swaps + list(loans.values()):
+    for s in range(4):
+        left = rs_recv.at[pl.ds(1, 16 if s else 15)]
+        pltpu.make_async_copy(left, left, ap_ssem.at[s]).wait()
+    for c in asks + answers + sends + swaps + list(loans.values()):
         c.wait_send()
 
 
@@ -347,10 +350,8 @@
             dma((4,)),
             dma((2,)),
             dma((2,)),
-            dma,
-            dma,
-            dma((3,)),
-            dma((3,)),
+            dma((4,)),
+            dma((4,)),
             dma((4,)),
             dma((4,)),
             dma((2,)),

time: 34.7 us -> 33.6 us (0.968)
  Pallas kernels: 33.9 us -> 32.9 us
    pallas_call x1, Pallas kernels: 33.9 us -> 32.9 us  [shards(): pl.pallas_call(functools.partial(kernel, scale), out_shape=jax.ShapeDtype...]
where the time goes in v5:
time: 33.6 us; the launch traced here: 33.5 us
  Pallas kernels  32.9 us (98%)
  local copies, waits for them, and re-layouts  0.66 us (2%)
    pallas_call x1, Pallas kernels, shards(): pl.pallas_call(functools.partial(kernel, scale), out_shape=jax.ShapeDtype...  32.9 us

profile of v5, /device:TPU:1, one launch (start us, length us, event | category | flops | bytes accessed | tf_op | source)
XLA Modules:
  0.0 33.5 jit_solution(2498671821612175282)
XLA Ops:
  0.0 32.9 %shard_map.73 = bf16[256,256]{1,0:T(8,128)(2,1)S(1)} custom-call(bf16[2048,256]{1,0:T(8,128)(2,1)} %feats_hbm.1, f32[3,2048]{1,0:T(4,128)} %pos_hbm.1, bf16[2,2048,128]{2,1,0:T(8,128)(2,1)} %phases_hbm.1, f32[128,256]{1,0:T(8,128)} %filt_hbm.1, bf16[256,256]{1,0:T(8,128)(2,1)} %w_hbm.1, s32[2,8]{1,0:T(2,128)} %tiles_hbm.1, s32[2]{0:T(128)} %count_hbm.1), custom_call_target="tpu_custom_call" | custom-call | tf_op jit(solution)/shard_map/pallas_call | solution.py:314
  32.9 0.7 %copy.9 = bf16[256,256]{1,0:T(8,128)(2,1)} copy(bf16[256,256]{1,0:T(8,128)(2,1)S(1)} %shard_map.73) | data formatting | bytes 262144

commit v6 on v5

--- a/solution.py
+++ b/solution.py
@@ -12,7 +12,7 @@
 TILE = 128
 CHUNKS = 2
 FAR = 1e30
-LATE = ((2, 1), (1, 0), (3, 0), (2, 0))
+LATE = ((2, 0),)
 ATOM_PEERS = [(i, j, k) for j in (4, 3, 5, 2, 6, 1, 7, 0) for i in (1, 0) for k in (1, 0) if i + j + k > 0]
 
 F32 = jnp.float32
@@ -39,6 +39,7 @@
     pos,
     ph,
     lent,
+    seen,
     filt,
     w,
     values,
@@ -62,6 +63,8 @@
     rs_rsem,
     ph_ssem,
     ph_rsem,
+    se_ssem,
+    se_rsem,
     rq_ssem,
     rq_rsem,
     sh_ssem,
@@ -241,52 +244,55 @@
         answers.append(remote(sh_send.at[i], sh_recv.at[i], sh_ssem.at[i], sh_rsem.at[i], (to, f)))
 
     answer(0, after)
+    answers[0].start()
     answer(1, before)
-
-    def term(hi, s, filtered):
-        if s == 0:
-            rows = pl.ds(pl.multiple_of((lax.rem(x_hi + hi, 2) * 4 + y) * 256, 256), 256)
-            return dot(ph[rows, :], filtered)
-        return dot(lent[3 - s, hi], filtered)
-
+    answers[1].start()
+
+    twin_rows = pl.ds(pl.multiple_of(((1 - x_hi) * 4 + y) * 256, 256), 256)
+    mate = (row * 2 + 1 - core, f)
+    shown = [remote(ph.at[twin_rows], seen.at[0], se_ssem.at[0], se_rsem.at[0], mate)]
+    shown[0].start()
     for j in (1, 3, 2):
         loans[j, 1].wait_recv()
+        s = 4 - j
+        shown.append(remote(lent.at[j - 1, 1], seen.at[s], se_ssem.at[s], se_rsem.at[s], mate))
+        shown[-1].start()
+
     swaps = []
-    first = None
-    for s in (0, 1, 3, 2):
+    here = there = None
+    for i, s in enumerate((0, 3, 1, 2)):
+        shown[i].wait_recv()
         arrived = rs_recv.at[pl.ds(1, 16 if s else 15)]
         pltpu.make_async_copy(arrived, arrived, ap_rsem.at[s]).wait()
-        swaps.append(remote(gat.at[core, s], gat.at[core, s], sw_ssem.at[s], sw_rsem.at[s], (row * 2 + 1 - core, f)))
-        swaps[-1].start()
-        part = term(1, s, gat[core, s].reshape(256, 128))
-        first = part if first is None else first + part
-    l_send[core] = first.astype(BF16)
-    sends = [remote(l_send.at[core], l_recv.at[core], l_ssem.at[0], l_rsem.at[0], (a, other))]
+        swaps.append(remote(gat.at[core, s], gat.at[core, s], sw_ssem.at[s], sw_rsem.at[s], mate))
+        swaps[i].start()
+        filtered = gat[core, s].reshape(256, 128)
+        part = dot(lent[3 - s, 1] if s else ph[twin_rows, :], filtered)
+        here = part if here is None else here + part
+        part = dot(seen[s], filtered)
+        there = part if there is None else there + part
+    l_send[0] = here.astype(BF16)
+    sends = [remote(l_send.at[0], l_recv.at[core], l_ssem.at[0], l_rsem.at[0], (a, other))]
     sends[0].start()
-    for c in answers:
-        c.start()
-    second = None
-    for s, swap in zip((0, 1, 3, 2), swaps):
-        swap.wait_recv()
-        part = term(1, s, gat[1 - core, s].reshape(256, 128))
-        second = part if second is None else second + part
-    l_send[1 - core] = second.astype(BF16)
-    sends.append(remote(l_send.at[1 - core], l_recv.at[1 - core], l_ssem.at[1], l_rsem.at[1], (a, other)))
+    l_send[1] = there.astype(BF16)
+    sends.append(remote(l_send.at[1], l_recv.at[core], l_ssem.at[1], l_rsem.at[1], (mate[0], other)))
     sends[1].start()
 
+    own_rows = pl.ds(pl.multiple_of(f * 256, 256), 256)
     mine = None
-    for s in (0, 1, 3, 2):
+    for s in (0, 3, 1, 2):
+        swaps[(0, 3, 1, 2).index(s)].wait_recv()
         if s:
             loans[4 - s, 0].wait_recv()
         both = jnp.concatenate([gat[0, s].reshape(256, 128), gat[1, s].reshape(256, 128)], axis=1)
-        part = term(0, s, both)
+        part = dot(lent[3 - s, 0] if s else ph[own_rows, :], both)
         mine = part if mine is None else mine + part
     l_own[...] = mine
 
     for c in answers:
         c.wait_recv()
     near = short[...] + sh_recv[0].astype(F32) + sh_recv[1].astype(F32)
-    own = feats[pl.ds(pl.multiple_of(f * 256, 256), 256), :].astype(F32)
+    own = feats[own_rows, :].astype(F32)
     l_own[...] = l_own[...] + near * (1.0 / math.sqrt(TILE)) + own
     for c in sends:
         c.wait_recv()
@@ -297,7 +303,7 @@
     for s in range(4):
         left = rs_recv.at[pl.ds(1, 16 if s else 15)]
         pltpu.make_async_copy(left, left, ap_ssem.at[s]).wait()
-    for c in asks + answers + sends + swaps + list(loans.values()):
+    for c in asks + answers + shown + sends + swaps + list(loans.values()):
         c.wait_send()
 
 
@@ -323,6 +329,7 @@
             vmem((3, 2048), F32),
             vmem((2048, 256), BF16),
             vmem((3, 2, 256, 256), BF16),
+            vmem((4, 256, 256), BF16),
             vmem((128, 256), F32),
             vmem((256, 256), BF16),
             vmem((2048, 256), BF16),
@@ -348,6 +355,8 @@
             dma((6,)),
             dma((4,)),
             dma((4,)),
+            dma((4,)),
+            dma((4,)),
             dma((2,)),
             dma((2,)),
             dma((4,)),

time: 33.6 us -> 33.5 us (level)
  no operation moved by 1% of the time
where the time goes in v6:
time: 33.5 us; the launch traced here: 33.4 us
  Pallas kernels  32.7 us (98%)
  local copies, waits for them, and re-layouts  0.66 us (2%)
    pallas_call x1, Pallas kernels, shards(): pl.pallas_call(functools.partial(kernel, scale), out_shape=jax.ShapeDtype...  32.7 us

profile of v6, /device:TPU:1, one launch (start us, length us, event | category | flops | bytes accessed | tf_op | source)
XLA Modules:
  0.0 33.4 jit_solution(16415795774747308148)
XLA Ops:
  0.0 32.7 %shard_map.73 = bf16[256,256]{1,0:T(8,128)(2,1)S(1)} custom-call(bf16[2048,256]{1,0:T(8,128)(2,1)} %feats_hbm.1, f32[3,2048]{1,0:T(4,128)} %pos_hbm.1, bf16[2,2048,128]{2,1,0:T(8,128)(2,1)} %phases_hbm.1, f32[128,256]{1,0:T(8,128)} %filt_hbm.1, bf16[256,256]{1,0:T(8,128)(2,1)} %w_hbm.1, s32[2,8]{1,0:T(2,128)} %tiles_hbm.1, s32[2]{0:T(128)} %count_hbm.1), custom_call_target="tpu_custom_call" | custom-call | tf_op jit(solution)/shard_map/pallas_call | solution.py:320
  32.8 0.7 %copy.9 = bf16[256,256]{1,0:T(8,128)(2,1)} copy(bf16[256,256]{1,0:T(8,128)(2,1)S(1)} %shard_map.73) | data formatting | bytes 262144

commit v7 on v6

--- a/solution.py
+++ b/solution.py
@@ -219,8 +219,8 @@
     gat[core, 0, x_lo, z] = (filt_share * share * scale).astype(BF16)
 
     y_at = [x_hi * 4 + lax.rem(y + j, 4) for j in range(4)]
-    for dz in (4, 3, 5, 2, 6, 1, 7, 0):
-        for j in (2, 1, 3, 0):
+    for j in (2, 1, 3, 0):
+        for dz in (4, 3, 5, 2, 6, 1, 7, 0):
             for i in (1, 0):
                 if dz + j + i > 0:
                     slot = (4 - j) % 4
@@ -271,12 +271,12 @@
         here = part if here is None else here + part
         part = dot(seen[s], filtered)
         there = part if there is None else there + part
+    l_send[1] = there.astype(BF16)
+    cross = remote(l_send.at[1], l_recv.at[core], l_ssem.at[1], l_rsem.at[1], (mate[0], other))
+    cross.start()
     l_send[0] = here.astype(BF16)
-    sends = [remote(l_send.at[0], l_recv.at[core], l_ssem.at[0], l_rsem.at[0], (a, other))]
+    sends = [remote(l_send.at[0], l_recv.at[core], l_ssem.at[0], l_rsem.at[0], (a, other)), cross]
     sends[0].start()
-    l_send[1] = there.astype(BF16)
-    sends.append(remote(l_send.at[1], l_recv.at[core], l_ssem.at[1], l_rsem.at[1], (mate[0], other)))
-    sends[1].start()
 
     own_rows = pl.ds(pl.multiple_of(f * 256, 256), 256)
     mine = None

time: 33.5 us -> 31.9 us (0.952)
  Pallas kernels: 32.7 us -> 31.1 us
    pallas_call x1, Pallas kernels: 32.7 us -> 31.1 us  [shards(): pl.pallas_call(functools.partial(kernel, scale), out_shape=jax.ShapeDtype...]
where the time goes in v7:
time: 31.9 us; the launch traced here: 31.8 us
  Pallas kernels  31.1 us (97%)
  local copies, waits for them, and re-layouts  0.66 us (2%)
    pallas_call x1, Pallas kernels, shards(): pl.pallas_call(functools.partial(kernel, scale), out_shape=jax.ShapeDtype...  31.1 us
    unnamed x1, local copies, waits for them, and re-layouts  0.66 us

profile of v7, /device:TPU:1, one launch (start us, length us, event | category | flops | bytes accessed | tf_op | source)
XLA Modules:
  0.0 31.8 jit_solution(5743719794722248902)
XLA Ops:
  0.0 31.1 %shard_map.73 = bf16[256,256]{1,0:T(8,128)(2,1)S(1)} custom-call(bf16[2048,256]{1,0:T(8,128)(2,1)} %feats_hbm.1, f32[3,2048]{1,0:T(4,128)} %pos_hbm.1, bf16[2,2048,128]{2,1,0:T(8,128)(2,1)} %phases_hbm.1, f32[128,256]{1,0:T(8,128)} %filt_hbm.1, bf16[256,256]{1,0:T(8,128)(2,1)} %w_hbm.1, s32[2,8]{1,0:T(2,128)} %tiles_hbm.1, s32[2]{0:T(128)} %count_hbm.1), custom_call_target="tpu_custom_call" | custom-call | tf_op jit(solution)/shard_map/pallas_call | solution.py:320
  31.1 0.7 %copy.9 = bf16[256,256]{1,0:T(8,128)(2,1)} copy(bf16[256,256]{1,0:T(8,128)(2,1)S(1)} %shard_map.73) | data formatting | bytes 262144

commit v8 on v7

--- a/solution.py
+++ b/solution.py
@@ -13,7 +13,7 @@
 CHUNKS = 2
 FAR = 1e30
 LATE = ((2, 0),)
-ATOM_PEERS = [(i, j, k) for j in (4, 3, 5, 2, 6, 1, 7, 0) for i in (1, 0) for k in (1, 0) if i + j + k > 0]
+ATOM_PEERS = [(i, j, k) for i in (1, 0) for j in (4, 3, 5, 2, 6, 1, 7, 0) for k in (1, 0) if i + j + k > 0]
 
 F32 = jnp.float32
 BF16 = jnp.bfloat16

time: 31.9 us -> 31.9 us (level)
  no operation moved by 1% of the time
where the time goes in v8:
time: 31.9 us; the launch traced here: 31.8 us
  Pallas kernels  31.1 us (97%)
  local copies, waits for them, and re-layouts  0.66 us (2%)
    pallas_call x1, Pallas kernels, shards(): pl.pallas_call(functools.partial(kernel, scale), out_shape=jax.ShapeDtype...  31.1 us
    unnamed x1, local copies, waits for them, and re-layouts  0.66 us

profile of v8, /device:TPU:1, one launch (start us, length us, event | category | flops | bytes accessed | tf_op | source)
XLA Modules:
  0.0 31.8 jit_solution(14493866789702507199)
XLA Ops:
  0.0 31.1 %shard_map.73 = bf16[256,256]{1,0:T(8,128)(2,1)S(1)} custom-call(bf16[2048,256]{1,0:T(8,128)(2,1)} %feats_hbm.1, f32[3,2048]{1,0:T(4,128)} %pos_hbm.1, bf16[2,2048,128]{2,1,0:T(8,128)(2,1)} %phases_hbm.1, f32[128,256]{1,0:T(8,128)} %filt_hbm.1, bf16[256,256]{1,0:T(8,128)(2,1)} %w_hbm.1, s32[2,8]{1,0:T(2,128)} %tiles_hbm.1, s32[2]{0:T(128)} %count_hbm.1), custom_call_target="tpu_custom_call" | custom-call | tf_op jit(solution)/shard_map/pallas_call | solution.py:320
  31.1 0.7 %copy.9 = bf16[256,256]{1,0:T(8,128)(2,1)} copy(bf16[256,256]{1,0:T(8,128)(2,1)S(1)} %shard_map.73) | data formatting | bytes 262144
